TPU v7x, 32 devices: a whole 2x2x4 slice. The times are simulated.
32 devices in a mesh: pairs: 8 (over z, y), gvec: 4 (over x, core).
Axes of the slice: x: 2, y: 2, z: 4, core: 2. Of those that a mesh axis runs over, the one named last changes fastest.
Arguments:
- elements: bfloat16 [16384, 3072], P('pairs', 'gvec'), may hold values from -0.3984375 to 0.3984375
- energy_index: int32 [16384], P('pairs'), may hold values from 0 to 63
Outputs:
- chi_window: float32 [192, 3072], P('pairs', 'gvec')
All inputs are finite; a program needn't handle non-finite values.
Results may differ from a plain program's by a relative error of at most 0.0018.
Values may be sent and summed in bfloat16 or wider, within the bound.
A program may use at most 64 MiB of HBM per device.

v0:
```python
import jax
import jax.numpy as jnp
from jax import lax
from jax.sharding import PartitionSpec as P

PW_DEV = 48
LEVELS = 64


def make_table():
    steps_k = jnp.arange(LEVELS, dtype=jnp.float32)
    delta = 0.2 * jnp.exp(steps_k * (jnp.log(jnp.float32(50.0)) / (LEVELS - 1)))
    return -2.0 / delta


def shards(elements, energy_index):
    table = make_table()
    levels_row = jnp.arange(LEVELS, dtype=jnp.int32)
    picked = (energy_index[:, None] == levels_row[None, :]).astype(jnp.float32)
    weight = jnp.sum(picked * table[None, :], axis=1)
    scaled = (weight[:, None] * elements.astype(jnp.float32)).astype(jnp.bfloat16)
    own_panel = elements[:, :PW_DEV]
    partial_tile = lax.dot_general(
        lax.all_gather(own_panel, "gvec", axis=1, tiled=True),
        scaled,
        (((0,), (0,)), ((), ())),
        preferred_element_type=jnp.float32,
    )
    return lax.psum_scatter(partial_tile, "pairs", scatter_dimension=0, tiled=True)


def solution(mesh):
    placed = (P("pairs", "gvec"), P("pairs"))
    return jax.shard_map(
        shards, mesh=mesh, in_specs=placed, out_specs=P("pairs", "gvec"), check_vma=False
    )
```

profile of v0, /device:TPU:0, one launch (start us, length us, event | category | flops | bytes accessed | tf_op | source)
XLA Modules:
  0.0 93.1 jit_solution(5193992976684688746)
XLA Ops:
  6.5 0.0 reduce-scatter.2.cloned.1.call-start
  6.6 1.1 %slice.3 = bf16[2048,48]{1,0:T(8,128)(2,1)S(1)} slice(bf16[2048,768]{1,0:T(8,128)(2,1)} %param.2), slice={[0:2048], [0:48]} | slice | bytes 393216 | tf_op jit(solution)/shard_map/slice | solution.py:22
  7.6 0.2 copy.5
  7.8 10.1 %all_gather.3 = bf16[2048,192]{0,1:T(8,128)(2,1)S(1)} all-gather(bf16[2048,48]{0,1:T(8,128)(2,1)S(1)} %copy.5), channel_id=1, replica_groups=mesh['pairs'=8,'gvec'=4] {'gvec'}, dimensions={1}, use_global_device_ids=true | all-gather | bytes 983040 | tf_op jit(solution)/shard_map/all_gather | solution.py:24
  17.9 0.9 select_reduce_fusion
  18.8 3.7 %fusion.2 = f32[192,768]{1,0:T(8,128)} fusion(bf16[2048,192]{0,1:T(8,128)(2,1)S(1)} %all_gather.3, bf16[2048,768]{1,0:T(8,128)(2,1)} %param.2, f32[2048]{0:T(1024)S(1)} %select_reduce_fusion), kind=kOutput, calls=%fused_computation.3 | convolution fusion | flops 608698368 | bytes 4530176 | tf_op jit(solution)/shard_map/dot_general | solution.py:23
  22.5 0.0 reduce-scatter.2.cloned.1.call-update
  22.5 63.8 %reduce-scatter.2.cloned.1.call-done = f32[24,768]{1,0:T(8,128)} async-done(((f32[192,768]{1,0:T(8,128)}), f32[24,768]{1,0:T(8,128)}) %reduce-scatter.2.cloned.1.call-update) | async-done | bytes 73744 | tf_op jit(solution)/shard_map/reduce_scatter | solution.py:29
  (1 shorter events, 0.0 us)
Async XLA Ops:
  6.5 79.7 %reduce-scatter.2.cloned.1.call-start = ((), (), s32[]{:S(2)}) async-start(), calls=%async_computation.1 | async-start | bytes 663552 | tf_op jit(solution)/shard_map/reduce_scatter | solution.py:29
Sparse Core Ops, SparseCore 0:
  22.6 63.5 reduce-scatter.1
where the time goes:
time: 93.3 us; the launch traced here: 93.1 us
  waiting for transfers between devices  63.8 us (68%)
  between operations  13.4 us (14%)
  blocking collectives  10.1 us (11%)
  matrix products  3.7 us (4%)
  local copies, waits for them, and re-layouts  1.28 us (1%)
    reduce_scatter x1, waiting for transfers between devices, shards(): lax.psum_scatter(partial_tile, 'pairs', scatter_dimension=0, tiled=True)  63.8 us
    all_gather x1, blocking collectives, shards(): lax.all_gather(own_panel, 'gvec', axis=1, tiled=True)  10.1 us
    dot_general x1, matrix products, shards(): lax.dot_general(lax.all_gather(own_panel, 'gvec', axis=1, tiled=True), sc...  3.7 us
  transfers between devices with their start and end apart: 1, of which 1 were waited for; matrix products, arithmetic and copies ran while one was open for 0% of the time, Pallas kernels for 0%

commit v1 on v0

v1 whole, which is shorter than its diff:
```python
import functools

import jax
import jax.numpy as jnp
from jax import lax
from jax.experimental import pallas as pl
from jax.experimental.pallas import tpu as pltpu
from jax.sharding import PartitionSpec as P

PW_DEV = 48
LEVELS = 64
MESH = pl.DeviceIdType.MESH


def weights_of(index):
    delta = 0.2 * jnp.exp(
        index.astype(jnp.float32) * (jnp.log(jnp.float32(50.0)) / (LEVELS - 1))
    )
    return -2.0 / delta


def kernel(
    n_pairs, n_gvec, el_hbm, idx_ref, out_ref,
    el, sc, panels, acc, own, sent, got,
    load_sem, gsend_sem, grecv_sem, ssend_sem, srecv_sem,
):
    pw = PW_DEV
    n_p, n_g = el.shape
    half = n_g // 2
    rows = n_gvec * pw // n_pairs
    n_chip = n_gvec // 2
    streamed = pw % rows == 0
    me_p, me_g = lax.axis_index("pairs"), lax.axis_index("gvec")
    chip, core = me_g // 2, lax.rem(me_g, 2)
    partner = chip * 2 + 1 - core

    barrier = pltpu.get_barrier_semaphore()
    for d in range(1, n_pairs):
        pl.semaphore_signal(
            barrier, inc=1, device_id=(lax.rem(me_p + d, n_pairs), me_g), device_id_type=MESH
        )
    for q in range(1, n_chip):
        pl.semaphore_signal(
            barrier, inc=1, device_id=(me_p, lax.rem(chip + q, n_chip) * 2 + core), device_id_type=MESH
        )
    pl.semaphore_signal(barrier, inc=1, device_id=(me_p, partner), device_id_type=MESH)

    stripe = pltpu.make_async_copy(el_hbm.at[:, :128], el.at[:, :128], load_sem.at[0])
    stripe.start()
    n_load = load_sem.shape[0] - 1
    step = n_p // n_load
    loads = []
    for k in range(n_load):
        at = pl.ds(k * step, step)
        loads.append(
            pltpu.make_async_copy(el_hbm.at[at, 128:], el.at[at, 128:], load_sem.at[1 + k])
        )
        loads[-1].start()

    weight = weights_of(idx_ref[...]).T

    def push(source, slot, to_g, n):
        return pltpu.make_async_remote_copy(
            src_ref=panels.at[source], dst_ref=panels.at[source],
            send_sem=gsend_sem.at[n], recv_sem=grecv_sem.at[slot],
            device_id=(me_p, to_g), device_id_type=MESH,
        )

    stripe.wait()
    for k in range(n_p // 128):
        at = pl.ds(k * 128, 128)
        panels[me_g, :, at] = el[at, :128].T[:pw]

    pl.semaphore_wait(barrier, n_pairs - 1 + n_chip)
    first = [push(me_g, me_g, lax.rem(chip + q, n_chip) * 2 + core, q) for q in range(1, n_chip)]
    first.append(push(me_g, me_g, partner, 0))
    for copy in first:
        copy.start()

    per = step // 128
    for k in range(n_p // 128):
        if k % per == 0:
            loads[k // per].wait()
        at = pl.ds(k * 128, 128)
        sc[at, :] = (weight[:, k:k + 1] * el[at, :].astype(jnp.float32)).astype(jnp.bfloat16)

    def send_to(to):
        return pltpu.make_async_remote_copy(
            src_ref=sent.at[to], dst_ref=got.at[me_p],
            send_sem=ssend_sem.at[to], recv_sem=srecv_sem.at[me_p],
            device_id=(to, me_g), device_id_type=MESH,
        )

    def emit(to, block):
        stacked = jnp.concatenate([block[:, :half], block[:, half:]], axis=0)

        @pl.when(to == me_p)
        def _():
            own[...] = stacked

        @pl.when(to != me_p)
        def _():
            sent[to] = stacked.astype(jnp.bfloat16)
            send_to(to).start()

    def tile_of(g):
        tile = jnp.dot(panels[g], sc[...], preferred_element_type=jnp.float32)
        if streamed:
            for b in range(pw // rows):
                emit(g * (pw // rows) + b, tile[b * rows:(b + 1) * rows])
        else:
            acc[pl.ds(pl.multiple_of(g * pw, 8), pw), :] = tile

    def arrived(g):
        push(g, g, partner, 0).wait_recv()

    tile_of(me_g)
    arrived(partner)
    tile_of(partner)

    def other_chip(q):
        g = lax.rem(chip + n_chip - q, n_chip) * 2
        arrived(g + core)
        push(g + core, g + core, partner, n_chip + q).start()
        tile_of(g + core)
        arrived(g + 1 - core)
        tile_of(g + 1 - core)

    if n_chip <= 2:
        for q in range(1, n_chip):
            other_chip(q)
    else:
        pl.loop(1, n_chip)(other_chip)
    if not streamed:
        for k in range(n_pairs):
            emit(k, acc[k * rows:(k + 1) * rows, :])

    total = own[...]
    for d in range(1, n_pairs):
        source = lax.rem(me_p + d, n_pairs)
        pltpu.make_async_remote_copy(
            src_ref=sent.at[source], dst_ref=got.at[source],
            send_sem=ssend_sem.at[source], recv_sem=srecv_sem.at[source],
            device_id=(source, me_g), device_id_type=MESH,
        ).wait_recv()
        total = total + got[source].astype(jnp.float32)
    out_ref[:, :half] = total[:rows]
    out_ref[:, half:] = total[rows:]

    for copy in first:
        copy.wait_send()
    for q in range(1, n_chip):
        push(me_g, me_g, partner, n_chip + q).wait_send()
    for d in range(1, n_pairs):
        send_to(lax.rem(me_p + d, n_pairs)).wait_send()


def shards(n_pairs, n_gvec, elements, energy_index):
    n_p, n_g = elements.shape
    rows = n_gvec * PW_DEV // n_pairs
    streamed = PW_DEV % rows == 0
    half = n_g // 2
    n_load = 8
    vmem = pltpu.VMEM
    dma = pltpu.SemaphoreType.DMA
    return pl.pallas_call(
        functools.partial(kernel, n_pairs, n_gvec),
        out_shape=jax.ShapeDtypeStruct((rows, n_g), jnp.float32),
        in_specs=[
            pl.BlockSpec(memory_space=pl.ANY),
            pl.BlockSpec(memory_space=vmem),
        ],
        out_specs=pl.BlockSpec(memory_space=vmem),
        scratch_shapes=[
            vmem((n_p, n_g), jnp.bfloat16),
            vmem((n_p, n_g), jnp.bfloat16),
            vmem((n_gvec, PW_DEV, n_p), jnp.bfloat16),
            vmem((8 if streamed else n_gvec * PW_DEV, n_g), jnp.float32),
            vmem((2 * rows, half), jnp.float32),
            vmem((n_pairs, 2 * rows, half), jnp.bfloat16),
            vmem((n_pairs, 2 * rows, half), jnp.bfloat16),
            dma((1 + n_load,)),
            dma((n_gvec,)),
            dma((n_gvec,)),
            dma((n_pairs,)),
            dma((n_pairs,)),
        ],
        compiler_params=pltpu.CompilerParams(collective_id=0, has_side_effects=True),
    )(elements, energy_index.reshape(n_p // 128, 128))


def solution(mesh):
    placed = (P("pairs", "gvec"), P("pairs"))
    body = functools.partial(shards, mesh.shape["pairs"], mesh.shape["gvec"])
    return jax.shard_map(
        body, mesh=mesh, in_specs=placed, out_specs=P("pairs", "gvec"), check_vma=False
    )
```

time: 93.3 us -> 20.8 us (0.22)
  the two profiles are of different devices: /device:TPU:0 before, /device:TPU:7 now
where the time goes in v1:
time: 20.8 us; the launch traced here: 20.6 us
  Pallas kernels  19.1 us (92%)
  local copies, waits for them, and re-layouts  1.52 us (7%)
    pallas_call x1, Pallas kernels, shards(): pl.pallas_call(functools.partial(kernel, n_pairs, n_gvec), out_shape=jax....  19.1 us
    unnamed x1, local copies, waits for them, and re-layouts  1.52 us

profile of v1, /device:TPU:7, one launch (start us, length us, event | category | flops | bytes accessed | tf_op | source)
XLA Modules:
  0.0 20.6 jit_solution(5430713272315710646)
XLA Ops:
  0.0 19.1 %shard_map.28 = f32[24,768]{1,0:T(8,128)} custom-call(bf16[2048,768]{1,0:T(8,128)(2,1)} %el_hbm.1, s32[16,128]{1,0:T(8,128)} %bitcast.1), custom_call_target="tpu_custom_call" | custom-call | tf_op jit(solution)/shard_map/pallas_call | solution.py:166
  19.1 1.5 %copy.4 = f32[24,768]{1,0:T(8,128)} copy(f32[24,768]{1,0:T(8,128)} %shard_map.28) | data formatting | bytes 147456

commit v2 on v1

--- a/solution.py
+++ b/solution.py
@@ -165,7 +165,7 @@
     dma = pltpu.SemaphoreType.DMA
     return pl.pallas_call(
         functools.partial(kernel, n_pairs, n_gvec),
-        out_shape=jax.ShapeDtypeStruct((rows, n_g), jnp.float32),
+        out_shape=pltpu.VMEM((rows, n_g), jnp.float32),
         in_specs=[
             pl.BlockSpec(memory_space=pl.ANY),
             pl.BlockSpec(memory_space=vmem),

time: 20.8 us -> 19.3 us (0.928)
  local copies, waits for them, and re-layouts: 1.52 us -> 0.64 us
  Pallas kernels: 19.1 us -> 18.5 us
    unnamed x1, local copies, waits for them, and re-layouts: 1.52 us -> 0.64 us
    pallas_call x1, Pallas kernels: 19.1 us -> 18.5 us  [shards(): pl.pallas_call(functools.partial(kernel, n_pairs, n_gvec), out_shape=pltp...]
where the time goes in v2:
time: 19.3 us; the launch traced here: 19.1 us
  Pallas kernels  18.5 us (96%)
  local copies, waits for them, and re-layouts  0.64 us (3%)
    pallas_call x1, Pallas kernels, shards(): pl.pallas_call(functools.partial(kernel, n_pairs, n_gvec), out_shape=pltp...  18.5 us
    unnamed x1, local copies, waits for them, and re-layouts  0.64 us

profile of v2, /device:TPU:7, one launch (start us, length us, event | category | flops | bytes accessed | tf_op | source)
XLA Modules:
  0.0 19.1 jit_solution(1053555592021938372)
XLA Ops:
  0.0 18.5 %shard_map.28 = f32[24,768]{1,0:T(8,128)S(1)} custom-call(bf16[2048,768]{1,0:T(8,128)(2,1)} %el_hbm.1, s32[16,128]{1,0:T(8,128)} %bitcast.1), custom_call_target="tpu_custom_call" | custom-call | tf_op jit(solution)/shard_map/pallas_call | solution.py:166
  18.5 0.6 %copy.4 = f32[24,768]{1,0:T(8,128)} copy(f32[24,768]{1,0:T(8,128)S(1)} %shard_map.28) | data formatting | bytes 147456

commit v3 on v2

--- a/solution.py
+++ b/solution.py
@@ -20,8 +20,8 @@
 
 
 def kernel(
-    n_pairs, n_gvec, el_hbm, idx_ref, out_ref,
-    el, sc, panels, acc, own, sent, got,
+    n_pairs, n_gvec, el_hbm, idx_hbm, out_ref,
+    idx, el, sc, panels, acc, own, sent, got,
     load_sem, gsend_sem, grecv_sem, ssend_sem, srecv_sem,
 ):
     pw = PW_DEV
@@ -30,34 +30,34 @@
     rows = n_gvec * pw // n_pairs
     n_chip = n_gvec // 2
     streamed = pw % rows == 0
+    index = pltpu.make_async_copy(idx_hbm, idx, load_sem.at[0])
     me_p, me_g = lax.axis_index("pairs"), lax.axis_index("gvec")
     chip, core = me_g // 2, lax.rem(me_g, 2)
     partner = chip * 2 + 1 - core
 
-    barrier = pltpu.get_barrier_semaphore()
-    for d in range(1, n_pairs):
-        pl.semaphore_signal(
-            barrier, inc=1, device_id=(lax.rem(me_p + d, n_pairs), me_g), device_id_type=MESH
-        )
-    for q in range(1, n_chip):
-        pl.semaphore_signal(
-            barrier, inc=1, device_id=(me_p, lax.rem(chip + q, n_chip) * 2 + core), device_id_type=MESH
-        )
-    pl.semaphore_signal(barrier, inc=1, device_id=(me_p, partner), device_id_type=MESH)
-
-    stripe = pltpu.make_async_copy(el_hbm.at[:, :128], el.at[:, :128], load_sem.at[0])
+    stripe = pltpu.make_async_copy(el_hbm.at[:, :128], el.at[:, :128], load_sem.at[1])
     stripe.start()
-    n_load = load_sem.shape[0] - 1
+    index.start()
+    n_load = load_sem.shape[0] - 2
     step = n_p // n_load
     loads = []
     for k in range(n_load):
         at = pl.ds(k * step, step)
         loads.append(
-            pltpu.make_async_copy(el_hbm.at[at, 128:], el.at[at, 128:], load_sem.at[1 + k])
+            pltpu.make_async_copy(el_hbm.at[at, 128:], el.at[at, 128:], load_sem.at[2 + k])
         )
         loads[-1].start()
 
-    weight = weights_of(idx_ref[...]).T
+    barrier = pltpu.get_barrier_semaphore()
+    for d in range(1, n_pairs):
+        pl.semaphore_signal(
+            barrier, inc=1, device_id=(lax.rem(me_p + d, n_pairs), me_g), device_id_type=MESH
+        )
+    for q in range(1, n_chip):
+        pl.semaphore_signal(
+            barrier, inc=1, device_id=(me_p, lax.rem(chip + q, n_chip) * 2 + core), device_id_type=MESH
+        )
+    pl.semaphore_signal(barrier, inc=1, device_id=(me_p, partner), device_id_type=MESH)
 
     def push(source, slot, to_g, n):
         return pltpu.make_async_remote_copy(
@@ -77,6 +77,8 @@
     for copy in first:
         copy.start()
 
+    index.wait()
+    weight = weights_of(idx[...]).T
     per = step // 128
     for k in range(n_p // 128):
         if k % per == 0:
@@ -168,10 +170,11 @@
         out_shape=pltpu.VMEM((rows, n_g), jnp.float32),
         in_specs=[
             pl.BlockSpec(memory_space=pl.ANY),
-            pl.BlockSpec(memory_space=vmem),
+            pl.BlockSpec(memory_space=pl.ANY),
         ],
         out_specs=pl.BlockSpec(memory_space=vmem),
         scratch_shapes=[
+            vmem((n_p // 128, 128), jnp.int32),
             vmem((n_p, n_g), jnp.bfloat16),
             vmem((n_p, n_g), jnp.bfloat16),
             vmem((n_gvec, PW_DEV, n_p), jnp.bfloat16),
@@ -179,7 +182,7 @@
             vmem((2 * rows, half), jnp.float32),
             vmem((n_pairs, 2 * rows, half), jnp.bfloat16),
             vmem((n_pairs, 2 * rows, half), jnp.bfloat16),
-            dma((1 + n_load,)),
+            dma((2 + n_load,)),
             dma((n_gvec,)),
             dma((n_gvec,)),
             dma((n_pairs,)),

time: 19.3 us -> 18.6 us (0.964)
  Pallas kernels: 18.5 us -> 17.8 us
    pallas_call x1, Pallas kernels: 18.5 us -> 17.8 us  [shards(): pl.pallas_call(functools.partial(kernel, n_pairs, n_gvec), out_shape=pltp...]
where the time goes in v3:
time: 18.6 us; the launch traced here: 18.5 us
  Pallas kernels  17.8 us (96%)
  local copies, waits for them, and re-layouts  0.64 us (3%)
    pallas_call x1, Pallas kernels, shards(): pl.pallas_call(functools.partial(kernel, n_pairs, n_gvec), out_shape=pltp...  17.8 us
    unnamed x1, local copies, waits for them, and re-layouts  0.64 us

profile of v3, /device:TPU:7, one launch (start us, length us, event | category | flops | bytes accessed | tf_op | source)
XLA Modules:
  0.0 18.5 jit_solution(5060273937490090130)
XLA Ops:
  0.0 17.8 %shard_map.28 = f32[24,768]{1,0:T(8,128)S(1)} custom-call(bf16[2048,768]{1,0:T(8,128)(2,1)} %el_hbm.1, s32[16,128]{1,0:T(8,128)} %bitcast.1), custom_call_target="tpu_custom_call" | custom-call | tf_op jit(solution)/shard_map/pallas_call | solution.py:168
  17.8 0.6 %copy.4 = f32[24,768]{1,0:T(8,128)} copy(f32[24,768]{1,0:T(8,128)S(1)} %shard_map.28) | data formatting | bytes 147456

commit v4 on v3

--- a/solution.py
+++ b/solution.py
@@ -46,7 +46,6 @@
         loads.append(
             pltpu.make_async_copy(el_hbm.at[at, 128:], el.at[at, 128:], load_sem.at[2 + k])
         )
-        loads[-1].start()
 
     barrier = pltpu.get_barrier_semaphore()
     for d in range(1, n_pairs):
@@ -67,6 +66,8 @@
         )
 
     stripe.wait()
+    for copy in loads:
+        copy.start()
     for k in range(n_p // 128):
         at = pl.ds(k * 128, 128)
         panels[me_g, :, at] = el[at, :128].T[:pw]
@@ -106,19 +107,27 @@
             send_to(to).start()
 
     def tile_of(g):
-        tile = jnp.dot(panels[g], sc[...], preferred_element_type=jnp.float32)
+        keep(g, jnp.dot(panels[g], sc[...], preferred_element_type=jnp.float32))
+
+    def keep(g, tile):
         if streamed:
             for b in range(pw // rows):
                 emit(g * (pw // rows) + b, tile[b * rows:(b + 1) * rows])
         else:
             acc[pl.ds(pl.multiple_of(g * pw, 8), pw), :] = tile
 
+    def pair_of(c):
+        tile = jnp.dot(
+            panels[pl.ds(c * 2, 2)].reshape(2 * pw, n_p), sc[...], preferred_element_type=jnp.float32
+        )
+        for n in range(2):
+            keep(c * 2 + n, tile[n * pw:(n + 1) * pw])
+
     def arrived(g):
         push(g, g, partner, 0).wait_recv()
 
-    tile_of(me_g)
     arrived(partner)
-    tile_of(partner)
+    pair_of(chip)
 
     def other_chip(q):
         g = lax.rem(chip + n_chip - q, n_chip) * 2

time: 18.6 us -> 18.6 us (level)
  no operation moved by 1% of the time
where the time goes in v4:
time: 18.6 us; the launch traced here: 18.4 us
  Pallas kernels  17.8 us (96%)
  local copies, waits for them, and re-layouts  0.64 us (3%)
    pallas_call x1, Pallas kernels, shards(): pl.pallas_call(functools.partial(kernel, n_pairs, n_gvec), out_shape=pltp...  17.8 us
    unnamed x1, local copies, waits for them, and re-layouts  0.64 us

profile of v4, /device:TPU:7, one launch (start us, length us, event | category | flops | bytes accessed | tf_op | source)
XLA Modules:
  0.0 18.4 jit_solution(14037651671650572800)
XLA Ops:
  0.0 17.8 %shard_map.28 = f32[24,768]{1,0:T(8,128)S(1)} custom-call(bf16[2048,768]{1,0:T(8,128)(2,1)} %el_hbm.1, s32[16,128]{1,0:T(8,128)} %bitcast.1), custom_call_target="tpu_custom_call" | custom-call | tf_op jit(solution)/shard_map/pallas_call | solution.py:177
  17.8 0.6 %copy.4 = f32[24,768]{1,0:T(8,128)} copy(f32[24,768]{1,0:T(8,128)S(1)} %shard_map.28) | data formatting | bytes 147456
